TPU v7x, 256 devices: a whole 4x4x8 slice. The times are simulated.
256 devices in a mesh: col: 128 (over x, z, y), sec: 2 (over core).
Axes of the slice: x: 4, y: 4, z: 8, core: 2. Of those that a mesh axis runs over, the one named last changes fastest.
Arguments:
- mps: bfloat16 [128, 96, 6, 6, 96], P('col', 'sec'), may hold values from -6 to 6
- ket: bfloat16 [128, 6, 6, 6, 6, 2], P('col'), may hold values from -6 to 6
- left_proj: bfloat16 [128, 96, 96, 6, 6], P('col', 'sec'), may hold values from -0.109375 to 0.109375
- right_proj: bfloat16 [128, 96, 6, 6, 96], P('col', None, None, None, 'sec'), may hold values from -0.109375 to 0.109375
- bond_charge: int32 [128, 96], P('col'), may hold values from 0 to 5
- new_charge: int32 [128, 96], P('col'), may hold values from 0 to 5
- link_charge: int32 [128, 6], P('col'), may hold values from 0 to 2
- vert_charge: int32 [128, 2, 6], P('col'), may hold values from 0 to 2
Outputs:
- new_mps: bfloat16 [128, 96, 6, 6, 96], P('col', 'sec')
- log_norm: float32 [], replicated
All inputs are finite; a program needn't handle non-finite values.
Results may differ from a plain program's by a relative error of at most 0.0064.
Values may be sent and summed in bfloat16 or wider, within the bound.
A program may use at most 192 MiB of HBM per device.

v0:
```python
import functools

import jax
import jax.numpy as jnp
from jax import lax
from jax.sharding import Mesh
from jax.sharding import PartitionSpec as P

COL = ("col_0", "col_1", "col_2")


def from_behind(x, axis, by):
    count = lax.axis_size(axis)
    return lax.ppermute(x, axis, [(i, (i + by) % count) for i in range(count)])


def joined_along(tiles, dim):
    tiles = jnp.moveaxis(tiles, 0, dim)
    shape = tiles.shape
    return tiles.reshape(*shape[:dim], shape[dim] * shape[dim + 1], *shape[dim + 2 :])


def copy_for_each(x, axis):
    count = lax.axis_size(axis)
    return lax.all_to_all(jnp.broadcast_to(x[None], (count, *x.shape)), axis, 0, 0, tiled=True)


def gather_directly(x, axis, dim):
    return joined_along(copy_for_each(x, axis), dim)


def gathered_total(x, axis):
    tiles = lax.all_gather(x, axis)
    return tiles.sum(axis=0)


def one_axis_at_a_time(x, axes):
    return functools.reduce(lax.psum, axes, x)


def absorb(
    mps_site,
    ket_site,
    left_site,
    right_site,
    charge_here,
    charge_next,
    fresh_here,
    fresh_next,
    link_here,
    link_next,
    vertical,
):
    upper = vertical[0]
    lower = vertical[1]
    physical = jnp.arange(ket_site.shape[4], dtype=jnp.int32)
    keep_mps = (
        charge_here[:, None, None, None] + upper[None, :, None, None] - upper[None, None, :, None]
        == charge_next[None, None, None, :]
    )
    masked_mps = jnp.where(keep_mps, mps_site, jnp.zeros_like(mps_site))
    keep_ket = (
        upper[:, None, None, None, None] + link_here[None, :, None, None, None]
        == lower[None, None, :, None, None]
        + link_next[None, None, None, :, None]
        + physical[None, None, None, None, :]
    )
    masked_ket = jnp.where(keep_ket, ket_site, jnp.zeros_like(ket_site))
    keep_left = (
        fresh_here[:, None, None, None]
        == charge_here[None, :, None, None]
        + link_here[None, None, :, None]
        - link_here[None, None, None, :]
    )
    masked_left = jnp.where(keep_left, left_site, jnp.zeros_like(left_site))
    keep_right = (
        charge_next[:, None, None, None]
        + link_next[None, :, None, None]
        - link_next[None, None, :, None]
        == fresh_next[None, None, None, :]
    )
    masked_right = jnp.where(keep_right, right_site, jnp.zeros_like(right_site))
    first = jnp.einsum(
        "xalm,auvb->xlmuvb", masked_left, masked_mps, preferred_element_type=jnp.float32
    ).astype(jnp.bfloat16)
    second = jnp.einsum(
        "xlmuvb,uldrp->xmvbdrp", first, masked_ket, preferred_element_type=jnp.float32
    ).astype(jnp.bfloat16)
    third = jnp.einsum(
        "xmvbdrp,vmesp->xbdres", second, masked_ket, preferred_element_type=jnp.float32
    ).astype(jnp.bfloat16)
    return jnp.einsum("xbdres,brsy->xdey", third, masked_right, preferred_element_type=jnp.float32)


def local(mps, ket, left_proj, right_proj, bond_charge, new_charge, link_charge, vert_charge):
    sites_here = mps.shape[0]
    half = left_proj.shape[1]
    full_mps = lax.all_gather(mps, "sec", axis=1, tiled=True)
    chi_full = full_mps.shape[1]
    legs = full_mps.shape[2]
    received = from_behind((bond_charge, new_charge, link_charge), COL, -1)
    bond_next = jnp.concatenate([bond_charge[1:], received[0]], axis=0)
    fresh_next = jnp.concatenate([new_charge[1:], received[1]], axis=0)
    link_next = jnp.concatenate([link_charge[1:], received[2]], axis=0)
    arrived = from_behind(right_proj, COL, -1)
    partial_next = jnp.concatenate([right_proj[1:], arrived], axis=0)
    right_next = gather_directly(partial_next, "sec", 4)
    offset = lax.axis_index("sec") * half
    fresh_half = lax.dynamic_slice_in_dim(new_charge[0], offset, half, 0)
    images = [
        absorb(
            full_mps[0],
            ket[0],
            left_proj[0],
            right_next[0],
            bond_charge[0],
            bond_next[0],
            fresh_half,
            fresh_next[0],
            link_charge[0],
            link_next[0],
            vert_charge[0],
        )
    ]
    image = jnp.stack(images, axis=0)
    partial_value = jnp.sum(image * image, axis=(1, 2, 3, 4))
    count = chi_full * legs * legs * chi_full
    columns = lax.axis_size(COL)
    squares = gathered_total(partial_value, "sec")
    meansq = squares / count
    logs = 0.5 * jnp.log(meansq + 1e-06)
    total = one_axis_at_a_time(jnp.sum(logs), COL)
    log_norm = total / (sites_here * columns)
    scale = lax.rsqrt(meansq + 1e-06)
    new_mps = (image * scale[:, None, None, None, None]).astype(jnp.bfloat16)
    return (new_mps, log_norm)


def solution(mesh):
    torus = Mesh(
        mesh.devices.reshape(4, 8, 4, mesh.shape["sec"]), ("col_0", "col_1", "col_2", "sec")
    )
    in_specs = (
        P(COL, "sec", None, None, None),
        P(COL, None, None, None, None, None),
        P(COL, "sec", None, None, None),
        P(COL, None, None, None, "sec"),
        P(COL, None),
        P(COL, None),
        P(COL, None),
        P(COL, None, None),
    )
    out_specs = (P(COL, "sec", None, None, None), P())
    return jax.shard_map(local, mesh=torus, in_specs=in_specs, out_specs=out_specs, check_vma=False)
```

profile of v0, /device:TPU:32, one launch (start us, length us, event | category | flops | bytes accessed | tf_op | source)
XLA Modules:
  0.0 162.3 jit_solution(1129275034538465947)
XLA Ops:
  0.6 2.6 %collective-permute-start = (s32[1,96]{1,0:T(1,128)}, s32[1,96]{1,0:T(1,128)S(1)}, u32[]{:S(2)}, u32[]{:S(2)}) collective-permute-start(s32[1,96]{1,0:T(1,128)} %param.12), channel_id=1, source_target_pairs={{0,254},{2,0},{4,2},{6,4},{8,6},{10,8},{12,10},{14,12},{16,14},{18... | collective-permute-start | bytes 1160 | tf_op jit(solution)/shard_map/ppermute | solution.py:14
  3.3 0.7 collective-permute-start.1
  4.0 0.4 collective-permute-start.3
  4.5 2.2 %collective-permute-start.2 = (s32[1,96]{1,0:T(1,128)}, s32[1,96]{1,0:T(1,128)S(1)}, u32[]{:S(2)}, u32[]{:S(2)}) collective-permute-start(s32[1,96]{1,0:T(1,128)} %param.13), channel_id=1, source_target_pairs={{0,254},{2,0},{4,2},{6,4},{8,6},{10,8},{12,10},{14,12},{16,14},{18... | collective-permute-start | bytes 1160 | tf_op jit(solution)/shard_map/ppermute | solution.py:14
  6.6 0.8 slice_bitcast_fusion
  7.4 0.7 broadcast_add_fusion.2
  8.1 0.7 broadcast_add_fusion.4
  8.8 0.1 broadcast_subtract_fusion.1
  8.9 0.7 dynamic-slice_bitcast_fusion
  9.6 0.7 broadcast_subtract_fusion.2
  10.4 4.4 %all_gather.9 = bf16[1,96,6,6,96]{4,1,3,2,0:T(8,128)(2,1)} all-gather(bf16[1,48,6,6,96]{4,1,3,2,0:T(8,128)(2,1)} %param.8), channel_id=1, replica_groups=mesh['col_0'=4,'col_1'=8,'col_2'=4,'sec'=2] {'sec'}, dimensions={1}, use_global_device_ids=true | all-gather | bytes 995328 | tf_op jit(solution)/shard_map/all_gather | solution.py:98
  14.7 1.3 dynamic-slice.1
  16.0 0.0 collective-permute-done.1
  16.0 0.1 broadcast_add_fusion.1
  16.1 1.1 fusion.29
  17.2 0.0 collective-permute-done
  17.2 5.8 %convert_bitcast_fusion = bf16[48,6,6,6,6,96,1,1]{5,0,4,3,2,1,7,6:T(8,128)(2,1)S(1)} fusion(bf16[1,96,6,6,96]{4,1,3,2,0:T(8,128)(2,1)} %all_gather.9, s32[96]{0:T(128)S(1)} %bitcast.67, s32[96,6,6]{0,2,1:T(8,128)S(1)} %broadcast_subtract_fusion.1, bf16[1,48,96,6,6]{2,1,4,3,0:T(8,128)(2,1)} %param.10, s32[96,6,6]{0,2,1:T(8,128)S(1)} %broadcast_subtract_fusion.2, ...), kind=kOutput, calls=%fused_computation.8 | convolution fusion | flops 1153585152 | bytes 12967488 | tf_op jit(solution)/shard_map/xalm,auvb->xlmuvb/dot_general | solution.py:83
  23.1 28.1 %fusion = bf16[48,6,6,96,6,6,2,1]{3,5,6,4,2,1,0,7:T(8,128)(2,1)} fusion(bf16[48,6,6,6,6,96,1,1]{5,0,4,3,2,1,7,6:T(8,128)(2,1)S(1)} %convert_bitcast_fusion, bf16[6,6,6,6,2,1,1,1]{3,4,2,1,0,7,6,5:T(2,128)(2,1)S(1)} %fusion.29), kind=kOutput, calls=%fused_computation.1 | convolution fusion | flops 871907328 | bytes 35836992 | tf_op jit(solution)/shard_map/xlmuvb,uldrp->xmvbdrp/dot_general | solution.py:86
  51.1 38.6 %bitcast_convert_fusion.1 = bf16[48,96,6,6,6,6]{1,5,4,3,2,0:T(8,128)(2,1)} fusion(bf16[48,6,6,96,6,6,2,1]{3,5,6,4,2,1,0,7:T(8,128)(2,1)} %fusion, bf16[6,6,6,6,2,1,1,1]{3,4,2,1,0,7,6,5:T(2,128)(2,1)S(1)} %fusion.29), kind=kOutput, calls=%fused_computation.2 | convolution fusion | flops 865935360 | bytes 35836992 | tf_op jit(solution)/shard_map/xmvbdrp,vmesp->xbdres/dot_general | solution.py:89
  89.7 0.1 broadcast_add_fusion
  89.8 0.1 broadcast_subtract_fusion
  89.8 0.0 collective-permute-done.3
  89.8 1.1 broadcast_in_dim.20
  91.0 4.5 %all_to_all.5 = bf16[2,1,96,6,6,48]{2,5,4,3,1,0:T(8,128)(2,1)S(1)} all-to-all(bf16[2,1,96,6,6,48]{2,5,4,3,1,0:T(8,128)(2,1)S(1)} %broadcast_in_dim.20), channel_id=1, replica_groups=mesh['col_0'=4,'col_1'=8,'col_2'=4,'sec'=2] {'sec'}, dimensions={0} | all-to-all | bytes 1327104 | tf_op jit(solution)/shard_map/all_to_all | solution.py:25
  95.5 0.1 copy.16
  95.6 0.0 collective-permute-done.2
  95.6 17.4 %multiply_reduce_fusion = (f32[]{:T(128)}, f32[48,6,6,96]{3,0,2,1:T(8,128)S(1)}) fusion(bf16[96,6,6,96]{0,3,2,1:T(8,128)(2,1)S(1)} %bitcast.60, s32[96,6,6]{0,2,1:T(8,128)S(1)} %broadcast_subtract_fusion, s32[96]{0:T(128)S(1)} %bitcast.70, bf16[48,96,6,6,6,6]{1,5,4,3,2,0:T(8,128)(2,1)} %bitcast_convert_fusion.1), kind=kOutput, calls=%fused_computation.15 | convolution fusion | flops 1147613184 | bytes 13285252 | tf_op jit(solution)/shard_map/xbdres,brsy->xdey/dot_general | solution.py:92
  112.9 1.4 dynamic-update-slice
  114.3 2.4 %all-reduce = f32[2]{0:T(128)S(1)} all-reduce(f32[2]{0:T(128)S(1)} %dynamic-update-slice), channel_id=1, replica_groups=mesh['col_0'=4,'col_1'=8,'col_2'=4,'sec'=2] {'sec'}, use_global_device_ids=true, to_apply=%add | all-reduce | flops 2 | bytes 16
  116.8 0.6 reduce.3
  118.1 9.3 %psum.21 = f32[]{:T(128)} all-reduce(f32[]{:T(128)S(6)} %mul.24), channel_id=1, replica_groups=mesh['col_0'=4,'col_1'=8,'col_2'=4,'sec'=2] {'col_0'}, use_global_device_ids=true, to_apply=%region_2.3 | all-reduce | flops 1 | bytes 8 | tf_op jit(solution)/shard_map/psum | solution.py:38
  127.4 20.9 %psum.22 = f32[]{:T(128)} all-reduce(f32[]{:T(128)} %psum.21), channel_id=1, replica_groups=mesh['col_0'=4,'col_1'=8,'col_2'=4,'sec'=2] {'col_1'}, use_global_device_ids=true, to_apply=%region_3.4 | all-reduce | flops 1 | bytes 8 | tf_op jit(solution)/shard_map/psum | solution.py:38
  148.3 11.4 %psum.23 = f32[]{:T(128)} all-reduce(f32[]{:T(128)} %psum.22), channel_id=1, replica_groups=mesh['col_0'=4,'col_1'=8,'col_2'=4,'sec'=2] {'col_2'}, use_global_device_ids=true, to_apply=%region_4.5 | all-reduce | flops 1 | bytes 8 | tf_op jit(solution)/shard_map/psum | solution.py:38
  159.7 0.8 fusion.21
  (2 shorter events, 0.0 us)
Async XLA Ops:
  0.6 16.6 %collective-permute-start = (s32[1,96]{1,0:T(1,128)}, s32[1,96]{1,0:T(1,128)S(1)}, u32[]{:S(2)}, u32[]{:S(2)}) collective-permute-start(s32[1,96]{1,0:T(1,128)} %param.12), channel_id=1, source_target_pairs={{0,254},{2,0},{4,2},{6,4},{8,6},{10,8},{12,10},{14,12},{16,14},{18... | collective-permute-start | bytes 1160 | tf_op jit(solution)/shard_map/ppermute | solution.py:14
  3.3 12.7 %collective-permute-start.1 = (s32[1,6]{1,0:T(1,128)}, s32[1,6]{1,0:T(1,128)S(1)}, u32[]{:S(2)}, u32[]{:S(2)}) collective-permute-start(s32[1,6]{1,0:T(1,128)} %param.14), channel_id=1, source_target_pairs={{0,254},{2,0},{4,2},{6,4},{8,6},{10,8},{12,10},{14,12},{16,14},{18... | collective-permute-start | bytes 80 | tf_op jit(solution)/shard_map/ppermute | solution.py:14
  4.0 85.8 %collective-permute-start.3 = (bf16[1,96,6,6,48]{1,4,3,2,0:T(8,128)(2,1)}, bf16[1,96,6,6,48]{1,4,3,2,0:T(8,128)(2,1)}, u32[]{:S(2)}, u32[]{:S(2)}) collective-permute-start(bf16[1,96,6,6,48]{1,4,3,2,0:T(8,128)(2,1)} %param.11), channel_id=1, source_target_pairs={{0,254},{2,0},{4,2},{6,4},{8,6},{10,8},{12,10},{14,12},{16,14},{18... | collective-permute-start | bytes 995336 | tf_op jit(solution)/shard_map/ppermute | solution.py:14
  4.5 91.1 %collective-permute-start.2 = (s32[1,96]{1,0:T(1,128)}, s32[1,96]{1,0:T(1,128)S(1)}, u32[]{:S(2)}, u32[]{:S(2)}) collective-permute-start(s32[1,96]{1,0:T(1,128)} %param.13), channel_id=1, source_target_pairs={{0,254},{2,0},{4,2},{6,4},{8,6},{10,8},{12,10},{14,12},{16,14},{18... | collective-permute-start | bytes 1160 | tf_op jit(solution)/shard_map/ppermute | solution.py:14
where the time goes:
time: 163 us; the launch traced here: 162 us
  matrix products  89.8 us (55%)
  blocking collectives  52.9 us (32%)
  starting transfers between devices  5.99 us (4%)
  local copies, waits for them, and re-layouts  5.34 us (3%)
  other arithmetic  5.05 us (3%)
  between operations  3.21 us (2%)
    psum x3, blocking collectives, one_axis_at_a_time(): return functools.reduce(lax.psum, axes, x)  41.6 us
    dot_general x1, matrix products, absorb(): jnp.einsum('xmvbdrp,vmesp->xbdres', second, masked_ket, preferred_element...  38.6 us
    dot_general x1, matrix products, absorb(): jnp.einsum('xlmuvb,uldrp->xmvbdrp', first, masked_ket, preferred_element_...  28.1 us
    dot_general x1, matrix products, absorb(): jnp.einsum('xbdres,brsy->xdey', third, masked_right, preferred_element_ty...  17.4 us
    ppermute x4, starting transfers between devices, from_behind(): return lax.ppermute(x, axis, [(i, (i + by) % count) for i in range(count)])  5.99 us
    dot_general x1, matrix products, absorb(): jnp.einsum('xalm,auvb->xlmuvb', masked_left, masked_mps, preferred_elemen...  5.81 us
    all_to_all x1, blocking collectives, copy_for_each(): lax.all_to_all(jnp.broadcast_to(x[None], (count, *x.shape)), axis, 0, 0,...  4.52 us
    all_gather x1, blocking collectives, local(): full_mps = lax.all_gather(mps, 'sec', axis=1, tiled=True)  4.38 us
  transfers between devices with their start and end apart: 4, of which 0 were waited for; matrix products, arithmetic and copies ran while one was open for 49% of the time, Pallas kernels for 0%

commit v1 on v0

v1 whole, which is shorter than its diff:
```python
import numpy as np

import jax
import jax.numpy as jnp
from jax import lax
from jax.experimental import pallas as pl
from jax.experimental.pallas import tpu as pltpu
from jax.sharding import Mesh
from jax.sharding import PartitionSpec as P

COL = ("col_0", "col_1", "col_2")
F32, BF16, I32 = jnp.float32, jnp.bfloat16, jnp.int32
MESH = pl.DeviceIdType.MESH
FORWARD_AT = 9


def operator_tables():
    e2 = np.zeros((432, 128), np.float32)
    f2 = np.zeros((48, 256), np.float32)
    k2 = np.zeros((432, 256), np.float32)
    rows_m = np.full(432, -1)
    cols_m = np.full(256, -2)
    for d in range(6):
        for r in range(6):
            for m in range(6):
                for p in range(2):
                    row = ((d * 6 + r) * 6 + m) * 2 + p
                    e2[row, (d * 6 + r) * 2 + p] = 1
                    rows_m[row] = m
    for u in range(6):
        for l in range(6):
            for m in range(6):
                f2[u * 6 + l, u * 40 + l * 6 + m] = 1
                cols_m[u * 40 + l * 6 + m] = m
    k2[:] = rows_m[:, None] == cols_m[None, :]
    e3 = np.zeros((2, 96, 128), np.float32)
    f3 = np.zeros((2, 48, 144), np.float32)
    rows_r = np.full(96, -1)
    cols_r = np.full(144, -2)
    for r in range(2):
        for s in range(6):
            for e in range(6):
                row = (r * 6 + s) * 8 + e
                rows_r[row] = r
                for p in range(2):
                    e3[p, row, (e * 6 + s) * 2 + p] = 1
        for v in range(6):
            for m in range(6):
                for p in range(2):
                    col = v * 24 + r * 12 + m * 2 + p
                    cols_r[col] = r
                    f3[p, v * 6 + m, col] = 1
    k3 = (rows_r[:, None] == cols_r[None, :]).astype(np.float32)
    gu = np.zeros((48, 128), np.float32)
    gl = np.zeros((48, 128), np.float32)
    for u in range(6):
        for l in range(6):
            gu[u * 6 + l, u] = 1
            gl[u * 6 + l, l] = 1
    hd = np.zeros((128, 128), np.float32)
    hr = np.zeros((128, 128), np.float32)
    hp = np.zeros((8, 128), np.float32)
    for d in range(6):
        for r in range(6):
            for p in range(2):
                hd[d, (d * 6 + r) * 2 + p] = 1
                hr[r, (d * 6 + r) * 2 + p] = 1
                hp[:, (d * 6 + r) * 2 + p] = p
    narrow = lambda t: jnp.asarray(t, BF16)
    return [narrow(e2), narrow(f2), jnp.asarray(k2), narrow(e3), narrow(f3), jnp.asarray(k3),
            jnp.asarray(gu), jnp.asarray(gl), narrow(hd), narrow(hr), jnp.asarray(hp)]


def column(row):
    return jnp.transpose(jnp.broadcast_to(row, (128, 128)))


def kernel(sizes, link_s, vert_s, bond, fresh, link, vert, ketm, e2, f2, k2, e3, f3, k3, gu, gl, hd, hr, hp,
           mps_h, left_h, right_h, out_h, log_out,
           rows, bond_n, fresh_n, link_n, left_v, MB, RB, LF, L2F, L2, MS, RS, KM, KB2, KB3, W1, W2, W3, IMG, OUT,
           SQ, SA, SB,
           lsem, csend, crecv, msend, mrecv, rsend, rrecv, fsend, frecv, qsend, qrecv, asend, arecv, bsend, brecv,
           osem):
    nx, nz, ny, _ = sizes
    x, z, y = lax.axis_index("col_0"), lax.axis_index("col_1"), lax.axis_index("col_2")
    sec = lax.axis_index("sec")
    other = 1 - sec
    count = nx * nz * ny
    site = (x * nz + z) * ny + y

    def place(j):
        return {"col_0": lax.div(j, nz * ny), "col_1": lax.rem(lax.div(j, ny), nz), "col_2": lax.rem(j, ny)}

    before = place(lax.rem(site + count - 1, count))
    after = place(lax.rem(site + 1, count))
    partner = {"sec": other}
    plane = x * ny + y
    plane_n = nx * ny

    def plane_peer(k):
        q = lax.rem(plane + k, plane_n)
        return {"col_0": lax.div(q, ny), "col_2": lax.rem(q, ny)}

    def line_peer(k):
        return {"col_1": lax.rem(z + k, nz)}

    left_copy = pltpu.make_async_copy(left_h, left_v, lsem.at[0])
    left_copy.start()
    mps_copy = pltpu.make_async_copy(mps_h, MB.at[sec], lsem.at[1])
    mps_copy.start()

    barrier = pltpu.get_barrier_semaphore()
    peers = [partner, before, after]
    peers += [plane_peer(k) for k in range(1, plane_n)]
    peers += [line_peer(k) for k in range(1, nz)]
    for peer in peers:
        pl.semaphore_signal(barrier, inc=1, device_id=peer, device_id_type=MESH)
    pl.semaphore_wait(barrier, len(peers))

    def remote(src, dst, send, recv, peer):
        return pltpu.make_async_remote_copy(src_ref=src, dst_ref=dst, send_sem=send, recv_sem=recv,
                                            device_id=peer, device_id_type=MESH)

    charges = [remote(bond, bond_n, csend.at[0], crecv.at[0], before),
               remote(fresh, fresh_n, csend.at[1], crecv.at[1], before),
               remote(link, link_n, csend.at[2], crecv.at[2], before)]
    for c in charges:
        c.start()
    mps_send = remote(mps_h, MB.at[sec], msend, mrecv, partner)
    mps_send.start()
    right_send = remote(right_h, RB.at[sec], rsend, rrecv, before)
    right_send.start()
    right_forward = remote(RB.at[sec], RB.at[sec], fsend, frecv, partner)

    rows[...] = jnp.zeros_like(rows)
    rows[0:1, 0:96] = bond[...]
    rows[1:2, 0:96] = fresh[...]
    qb = rows[0:1, :]
    col_qb = column(qb)
    col_fresh = column(rows[1:2, :])
    LF[...] = jnp.zeros_like(LF)
    L2F[...] = jnp.zeros_like(L2F)
    fresh_half = jnp.where(sec == 0, col_fresh[0:48, :], col_fresh[48:96, :])
    left_diff = fresh_half[:, :96] - qb[:, :96]
    left_copy.wait()
    for l in range(6):
        for m in range(6):
            keep = left_diff == link_s[0, l] - link_s[0, m]
            LF[pl.ds((l * 6 + m) * 48, 48), 0:96] = jnp.where(keep, left_v[l, m].astype(F32), 0.0)
    for i in range(48):
        L2F[pl.ds(40 * i, 36), :] = LF[pl.ds(i, 36, stride=48), :]
    L2[...] = L2F[...].astype(BF16)
    W1[:, :, 240:256, :] = jnp.zeros((24, 6, 16, 256), BF16)
    MS[...] = jnp.zeros_like(MS)
    RS[...] = jnp.zeros_like(RS)
    KM[...] = jnp.zeros_like(KM)

    for c in charges:
        c.wait_recv()
    rows[2:3, 0:96] = bond_n[...]
    rows[3:4, 0:96] = fresh_n[...]
    rows[4:5, 0:6] = link[...]
    rows[5:6, 0:6] = link_n[...]
    rows[6:8, 0:6] = vert[0]
    qbn = rows[2:3, :]

    charge_rows = rows[...].astype(F32)
    ket_rows = jnp.sum(gu[...] * charge_rows[6:7, :] + gl[...] * charge_rows[4:5, :], axis=1, keepdims=True)
    lower = jnp.broadcast_to(charge_rows[7:8, :], (8, 128)).astype(BF16)
    ahead = jnp.broadcast_to(charge_rows[5:6, :], (8, 128)).astype(BF16)
    ket_cols = (jnp.dot(lower, hd[...], preferred_element_type=F32)
                + jnp.dot(ahead, hr[...], preferred_element_type=F32) + hp[...])[0:1, :]
    keep_ket = jnp.abs(ket_rows - ket_cols) < 0.5
    KM[0:36, 0:72] = jnp.where(keep_ket[0:36, 0:72], ketm[...].astype(F32), 0.0).astype(BF16)
    spread = lax.dot_general(e2[...], KM[...], (((1,), (1,)), ((), ())), preferred_element_type=F32)
    KB2[...] = (jnp.dot(spread.astype(BF16), f2[...], preferred_element_type=F32) * k2[...]).astype(BF16)
    total = None
    for p in range(2):
        spread = lax.dot_general(e3[p], KM[...], (((1,), (1,)), ((), ())), preferred_element_type=F32)
        part = jnp.dot(spread.astype(BF16), f3[p], preferred_element_type=F32)
        total = part if total is None else total + part
    KB3[...] = (total * k3[...]).astype(BF16)

    bond_diff = qbn[:, :96] - col_qb[:96, :96]
    mps_copy.wait()
    mps_send.wait_recv()
    for u in range(6):
        for v in range(6):
            keep = bond_diff == vert_s[0, 0, u] - vert_s[0, 0, v]
            t = jnp.concatenate([MB[0, u, v], MB[1, u, v]], axis=0).astype(F32)
            MS[(u // 2) * 6 + v, 0:96, pl.ds((u % 2) * 128, 96)] = jnp.where(keep, t, 0.0).astype(BF16)

    def step1(i, carry):
        up, v = lax.div(i, 6), lax.rem(i, 6)
        rhs = MS[i]
        for c in range(12):
            o = jnp.dot(L2[c * 160:(c + 1) * 160, :], rhs, preferred_element_type=F32)
            for k in range(4):
                s = 4 * c + k
                t = jnp.concatenate([o[40 * k:40 * k + 40, :128], o[40 * k:40 * k + 40, 128:]], axis=0)
                W1[s // 2, v, pl.ds(pl.multiple_of(up * 80, 16), 80),
                   (s % 2) * 128:(s % 2) * 128 + 128] = t.astype(BF16)
        return carry

    lax.fori_loop(0, 18, step1, 0)

    def do2(xp, slot):
        for vp in range(3):
            oa = jnp.dot(KB2[...], W1[xp, 2 * vp], preferred_element_type=F32)
            ob = jnp.dot(KB2[...], W1[xp, 2 * vp + 1], preferred_element_type=F32)
            for g in range(18):
                t = jnp.concatenate([oa[24 * g:24 * g + 24], ob[24 * g:24 * g + 24]], axis=0)
                W2[slot, g, 48 * vp:48 * vp + 48, :] = t.astype(BF16)

    def do3(xp, slot):
        for g in range(18):
            d, rp = g // 3, g % 3
            o = jnp.dot(KB3[...], W2[slot, g], preferred_element_type=F32)
            for i in range(12):
                rs = (2 * rp + i // 6) * 6 + i % 6
                t = jnp.concatenate([o[8 * i:8 * i + 8, :128], o[8 * i:8 * i + 8, 128:]], axis=0)
                W3[pl.ds(pl.multiple_of(xp * 96 + d * 16, 16), 16), rs * 128:rs * 128 + 128] = t.astype(BF16)

    do2(0, 0)

    def step23(xp, carry):
        slot = lax.rem(xp, 2)

        @pl.when(xp == FORWARD_AT)
        def _():
            right_send.wait_recv()
            right_forward.start()

        do2(xp, slot)
        do3(xp - 1, 1 - slot)
        return carry

    lax.fori_loop(1, 24, step23, 0)
    do3(23, 1)

    right_forward.wait_recv()
    col_qy = column(rows[3:4, :])
    right_diff = col_qy[:96, :96] - qbn[:, :96]
    ahead_row = rows[5:6, :]
    for r in range(6):
        for s in range(6):
            keep = right_diff == ahead_row[:, r:r + 1] - ahead_row[:, s:s + 1]
            t = jnp.concatenate([RB[0, r, s], RB[1, r, s]], axis=0).astype(F32)
            rs = r * 6 + s
            RS[:, rs * 128:rs * 128 + 96] = jnp.where(keep, t, 0.0).astype(BF16)

    def step4(c, acc):
        o = lax.dot_general(W3[pl.ds(pl.multiple_of(c * 384, 128), 384), :], RS[...],
                            (((1,), (1,)), ((), ())), preferred_element_type=F32)
        for k in range(4):
            for d in range(6):
                for h in range(2):
                    row = (c * 8 + 2 * k + h) * 48 + d * 8
                    at = k * 96 + d * 16 + h * 8
                    tile = o[at:at + 8]
                    IMG[pl.ds(pl.multiple_of(row, 8), 8), 0:96] = tile
                    acc = acc + tile * tile
        return acc

    acc = lax.fori_loop(0, 6, step4, jnp.zeros((8, 96), F32))
    mine = jnp.sum(jnp.sum(acc, axis=0, keepdims=True), axis=1, keepdims=True)
    SQ[sec] = jnp.broadcast_to(mine, (1, 128))
    square_send = remote(SQ.at[sec], SQ.at[sec], qsend, qrecv, partner)
    square_send.start()
    square_send.wait_recv()
    meansq = (SQ[0] + SQ[1]) / 331776.0
    scale = lax.rsqrt(meansq + 1e-06)
    SA[plane] = 0.5 * jnp.log(meansq + 1e-06)

    plane_sends = [remote(SA.at[plane], SA.at[plane], asend.at[k], arecv.at[k], plane_peer(k))
                   for k in range(1, plane_n)]
    for c in plane_sends:
        c.start()

    for d in range(6):
        for e in range(6):
            t = IMG[pl.ds(d * 8 + e, 48, stride=48), 0:96]
            OUT[d, e] = (t * scale[:, 0:96]).astype(BF16)
    out_copy = pltpu.make_async_copy(OUT, out_h, osem)
    out_copy.start()

    for c in plane_sends:
        c.wait_recv()
    total = SA[0]
    for k in range(1, plane_n):
        total = total + SA[k]
    SB[z] = total
    line_sends = [remote(SB.at[z], SB.at[z], bsend.at[k], brecv.at[k], line_peer(k)) for k in range(1, nz)]
    for c in line_sends:
        c.start()
    for c in line_sends:
        c.wait_recv()
    total = SB[0]
    for k in range(1, nz):
        total = total + SB[k]
    log_out[...] = total / float(count)

    for c in charges + [mps_send, right_send, right_forward, square_send] + plane_sends + line_sends:
        c.wait_send()
    out_copy.wait()


def local(sizes, mps, ket, left_proj, right_proj, bond_charge, new_charge, link_charge, vert_charge):
    nx, nz, ny, _ = sizes
    mps_v = mps[0].transpose(1, 2, 0, 3)
    left_v = left_proj[0].transpose(2, 3, 0, 1)
    right_v = right_proj[0].transpose(1, 2, 3, 0)
    ketm = ket.reshape(36, 72)
    tables = operator_tables()
    vm = pl.BlockSpec(memory_space=pltpu.VMEM)
    sm = pl.BlockSpec(memory_space=pltpu.SMEM)
    hbm = pl.BlockSpec(memory_space=pl.ANY)
    dma = pltpu.SemaphoreType.DMA
    out, log_row = pl.pallas_call(
        lambda *refs: kernel(sizes, *refs),
        out_shape=(jax.ShapeDtypeStruct((6, 6, 48, 96), BF16), jax.ShapeDtypeStruct((1, 128), F32)),
        in_specs=[sm, sm] + [vm] * (5 + len(tables)) + [hbm] * 3,
        out_specs=(hbm, vm),
        scratch_shapes=[
            pltpu.VMEM((8, 128), I32),
            pltpu.VMEM((1, 96), I32), pltpu.VMEM((1, 96), I32), pltpu.VMEM((1, 6), I32),
            pltpu.VMEM((6, 6, 48, 96), BF16),
            pltpu.VMEM((2, 6, 6, 48, 96), BF16), pltpu.VMEM((2, 6, 6, 48, 96), BF16),
            pltpu.VMEM((1728, 128), F32), pltpu.VMEM((1920, 128), F32), pltpu.VMEM((1920, 128), BF16),
            pltpu.VMEM((18, 128, 256), BF16), pltpu.VMEM((96, 4608), BF16),
            pltpu.VMEM((48, 128), BF16), pltpu.VMEM((432, 256), BF16), pltpu.VMEM((96, 144), BF16),
            pltpu.VMEM((24, 6, 256, 256), BF16), pltpu.VMEM((2, 18, 144, 256), BF16),
            pltpu.VMEM((2304, 4608), BF16), pltpu.VMEM((2304, 128), F32),
            pltpu.VMEM((6, 6, 48, 96), BF16),
            pltpu.VMEM((2, 1, 128), F32), pltpu.VMEM((nx * ny, 1, 128), F32), pltpu.VMEM((nz, 1, 128), F32),
            dma((2,)), dma((3,)), dma((3,)), dma(()), dma(()), dma(()), dma(()), dma(()), dma(()), dma(()), dma(()),
            dma((nx * ny,)), dma((nx * ny,)), dma((nz,)), dma((nz,)), dma(())],
        compiler_params=pltpu.CompilerParams(
            vmem_limit_bytes=67_043_328, collective_id=0, has_side_effects=True),
    )(link_charge, vert_charge, bond_charge, new_charge, link_charge, vert_charge, ketm, *tables,
      mps_v, left_v, right_v)
    return out.transpose(2, 0, 1, 3)[None], log_row[0, 0]


def solution(mesh):
    if mesh.shape["col"] == 128:
        sizes = (4, 8, 4, mesh.shape["sec"])
    else:
        sizes = (2, mesh.shape["col"] // 4, 2, mesh.shape["sec"])
    torus = Mesh(mesh.devices.reshape(sizes), (*COL, "sec"))
    in_specs = (
        P(COL, "sec", None, None, None),
        P(COL, None, None, None, None, None),
        P(COL, "sec", None, None, None),
        P(COL, None, None, None, "sec"),
        P(COL, None),
        P(COL, None),
        P(COL, None),
        P(COL, None, None),
    )
    out_specs = (P(COL, "sec", None, None, None), P())
    return jax.shard_map(lambda *a: local(sizes, *a), mesh=torus, in_specs=in_specs, out_specs=out_specs,
                         check_vma=False)
```

time: 163 us -> 70 us (0.43)
  matrix products: 89.8 us -> 0 us
  Pallas kernels: 0 us -> 62.9 us
  blocking collectives: 52.9 us -> 0 us
  starting transfers between devices: 5.99 us -> 0 us
  other arithmetic: 5.05 us -> 0 us
    dot_general x4 -> x0, matrix products: 89.8 us -> none  [the longest x1 38.6 us: absorb(): jnp.einsum('xmvbdrp,vmesp->xbdres', second, masked_ket, preferred_element...]
    pallas_call x0 -> x1, Pallas kernels: none -> 62.9 us  [local(): pl.pallas_call(lambda *refs: kernel(sizes, *refs), out_shape=(jax.ShapeDt...]
    psum x3 -> x0, blocking collectives: 41.6 us -> none  [one_axis_at_a_time(): return functools.reduce(lax.psum, axes, x)]
    ppermute x4 -> x0, starting transfers between devices: 5.99 us -> none  [from_behind(): return lax.ppermute(x, axis, [(i, (i + by) % count) for i in range(count)])]
    all_to_all x1 -> x0, blocking collectives: 4.52 us -> none  [copy_for_each(): lax.all_to_all(jnp.broadcast_to(x[None], (count, *x.shape)), axis, 0, 0,...]
    all_gather x1 -> x0, blocking collectives: 4.38 us -> none  [local(): full_mps = lax.all_gather(mps, 'sec', axis=1, tiled=True)]
    unnamed x1 -> x0, blocking collectives: 2.45 us -> none
    unnamed x3 -> x4, local copies, waits for them, and re-layouts: 2.66 us -> 3.46 us
  transfers between devices with their start and end apart: 4 -> 0, of which waited for: 0 -> 0; matrix products, arithmetic and copies ran while one was open for 49% -> 0% of each run, Pallas kernels for 0% -> 0%
where the time goes in v1:
time: 70 us; the launch traced here: 69 us
  Pallas kernels  62.9 us (90%)
  local copies, waits for them, and re-layouts  4.3 us (6%)
  between operations  1.82 us (3%)
    pallas_call x1, Pallas kernels, local(): pl.pallas_call(lambda *refs: kernel(sizes, *refs), out_shape=(jax.ShapeDt...  62.9 us
    unnamed x4, local copies, waits for them, and re-layouts  3.46 us

profile of v1, /device:TPU:32, one launch (start us, length us, event | category | flops | bytes accessed | tf_op | source)
XLA Modules:
  0.0 69.0 jit_solution(13840212804060609491)
XLA Ops:
  0.6 1.6 %copy.22 = bf16[1,6,6,6,6,2]{2,1,5,4,3,0:T(8,128)(2,1)S(1)} copy(bf16[1,6,6,6,6,2]{4,5,3,2,1,0:T(2,128)(2,1)} %param.20) | data formatting | bytes 10368 | tf_op args[1]
  2.3 0.1 reshape.7
  2.4 0.7 %copy.23.refs_6_ = bf16[36,72]{1,0:T(8,128)(2,1)} copy(bf16[36,72]{0,1:T(8,128)(2,1)S(1)} %reshape.7) | data formatting | bytes 10368 | tf_op jit(solution)/shard_map/reshape | solution.py:313
  3.1 62.9 %shard_map.194 = (bf16[6,6,48,96]{3,2,1,0:T(8,128)(2,1)}, f32[1,128]{1,0:T(1,128)}) custom-call(s32[1,6]{1,0:T(1,128)} %refs_4_.1, s32[1,2,6]{2,1,0:T(2,128)} %refs_5_.1, s32[1,96]{1,0:T(1,128)} %refs_2_.1, s32[1,96]{1,0:T(1,128)} %refs_3_.1, s32[1,6]{1,0:T(1,128)} %refs_4_.1, s32[1,2,6]{2,1,0:T(2,128)} %refs_5_.1, bf16[36,72]{1,0:T(8,128)(2,1)} %copy.23.refs_6_, ...), custom_call_target="tpu_custom_call" | custom-call | tf_op jit(solution)/shard_map/pallas_call | solution.py:319
  66.0 0.0 copy-start
  66.0 1.8 %copy.26 = bf16[1,48,6,6,96]{4,1,3,2,0:T(8,128)(2,1)} copy(bf16[1,48,6,6,96]{4,1,3,2,0:T(8,128)(2,1)} %bitcast.19) | data formatting | bytes 663552
  67.8 0.0 copy-done
Async XLA Ops:
  66.0 1.8 %copy-start = (f32[1,128]{1,0:T(1,128)S(1)}, f32[1,128]{1,0:T(1,128)}, u32[]{:S(2)}) copy-start(f32[1,128]{1,0:T(1,128)} %get-tuple-element.5) | copy-start | bytes 1540

commit v2 on v1

v2 whole, which is shorter than its diff:
```python
import numpy as np

import jax
import jax.numpy as jnp
from jax import lax
from jax.experimental import pallas as pl
from jax.experimental.pallas import tpu as pltpu
from jax.sharding import Mesh
from jax.sharding import PartitionSpec as P

COL = ("col_0", "col_1", "col_2")
F32, BF16, I32 = jnp.float32, jnp.bfloat16, jnp.int32
MESH = pl.DeviceIdType.MESH
FORWARD_AT = 3
CHUNK1 = 480
VMEM_LIMIT = 67_043_328


def operator_tables():
    e2 = np.zeros((432, 128), np.float32)
    f2 = np.zeros((48, 256), np.float32)
    rows_m = np.full(432, -1)
    cols_m = np.full(256, -2)
    hd = np.zeros((128, 128), np.float32)
    hr = np.zeros((128, 128), np.float32)
    hp = np.zeros((16, 128), np.float32)
    for d in range(6):
        for r in range(6):
            for p in range(2):
                lane = (2 * d + p) * 8 + r
                hd[d, lane] = 1
                hr[r, lane] = 1
                hp[:, lane] = p
                for m in range(6):
                    row = ((d * 6 + r) * 6 + m) * 2 + p
                    e2[row, lane] = 1
                    rows_m[row] = m
    gu = np.zeros((48, 128), np.float32)
    gl = np.zeros((48, 128), np.float32)
    for u in range(6):
        for l in range(6):
            gu[u * 6 + l, u] = 1
            gl[u * 6 + l, l] = 1
            for m in range(6):
                f2[u * 6 + l, u * 40 + l * 6 + m] = 1
                cols_m[u * 40 + l * 6 + m] = m
    k2 = rows_m[:, None] == cols_m[None, :]
    e3 = np.zeros((2, 96, 128), np.float32)
    f3 = np.zeros((2, 48, 256), np.float32)
    rows_r = np.full(96, -1)
    cols_r = np.full(256, -2)
    for r in range(2):
        for s in range(6):
            for e in range(6):
                row = (r * 6 + s) * 8 + e
                rows_r[row] = r
                for p in range(2):
                    e3[p, row, (2 * e + p) * 8 + s] = 1
        for v in range(6):
            for m in range(6):
                for p in range(2):
                    col = v * 24 + r * 12 + m * 2 + p
                    cols_r[col] = r
                    f3[p, v * 6 + m, col] = 1
    k3 = rows_r[:, None] == cols_r[None, :]
    narrow = np.concatenate([e2, e3.reshape(192, 128), hd, hr, gu, gl, hp])
    wide = np.concatenate([f2, k2, f3.reshape(96, 256), k3])
    return jnp.asarray(narrow, BF16), jnp.asarray(wide, BF16)


def column(row):
    return jnp.transpose(jnp.broadcast_to(row, (128, 128)))


def lane_parts(t):
    lane = lax.broadcasted_iota(I32, (96, 128), 1)
    t = jnp.concatenate([t, jnp.zeros((96, 32), F32)], axis=1)
    r32, r64, r96 = (pltpu.roll(t, n, axis=1) for n in (32, 64, 96))
    first = [t, jnp.where(lane < 64, r96, 0.0), jnp.where(lane < 32, r64, 0.0)]
    second = [jnp.where(lane >= 96, r96, 0.0), jnp.where(lane >= 64, r64, 0.0), jnp.where(lane >= 32, r32, 0.0)]
    return first, second


def kernel(sizes, bond, fresh, link, vert, narrow_h, wide_h, ket_h, mps_h, left_h, right_h, out_h, log_out,
           rows, bond_v, fresh_v, link_v, vert_v, bond_n, fresh_n, link_n, link_s, vert_s,
           narrow, wide, KH, KF, left_v, MB, RB, LF, L2F, L2, MS, RS, KM, KB2, KB3, W1, W2, W3, O4, IMG, OUT,
           SA, SB,
           lsem, csend, crecv, msend, mrecv, rsend, rrecv, fsend, frecv, asend, arecv, bsend, brecv, osem):
    nx, nz, ny, _ = sizes
    x, z, y = lax.axis_index("col_0"), lax.axis_index("col_1"), lax.axis_index("col_2")
    sec = lax.axis_index("sec")
    other = 1 - sec
    count = nx * nz * ny
    site = (x * nz + z) * ny + y

    def place(j):
        return {"col_0": lax.div(j, nz * ny), "col_1": lax.rem(lax.div(j, ny), nz), "col_2": lax.rem(j, ny)}

    before = place(lax.rem(site + count - 1, count))
    after = place(lax.rem(site + 1, count))
    partner = {"sec": other}
    plane = x * ny + y
    plane_n = nx * ny

    def plane_peer(k, flip):
        q = lax.rem(plane + k, plane_n)
        return {"col_0": lax.div(q, ny), "col_2": lax.rem(q, ny), "sec": other if flip else sec}

    def line_peer(k):
        return {"col_1": lax.rem(z + k, nz)}

    barrier = pltpu.get_barrier_semaphore()
    peers = [before, after]
    peers += [plane_peer(k, f) for k in range(plane_n) for f in range(2) if k + f > 0]
    peers += [line_peer(k) for k in range(1, nz)]
    for peer in peers:
        pl.semaphore_signal(barrier, inc=1, device_id=peer, device_id_type=MESH)

    fetched = [pltpu.make_async_copy(src, dst, lsem.at[i]) for i, (src, dst) in enumerate([
        (link, link_s), (bond, bond_v), (fresh, fresh_v), (left_h, left_v), (vert, vert_s), (link, link_v),
        (vert, vert_v), (ket_h, KH), (narrow_h, narrow), (wide_h, wide), (mps_h, MB.at[sec])])]
    for c in fetched:
        c.start()

    rows[...] = jnp.zeros_like(rows)
    LF[...] = jnp.zeros_like(LF)
    L2F[...] = jnp.zeros_like(L2F)
    MS[:, :, 96:128, :] = jnp.zeros((3, 3, 32, 512), BF16)
    MS[:, :, 224:256, :] = jnp.zeros((3, 3, 32, 512), BF16)
    KF[...] = jnp.zeros_like(KF)
    KM[...] = jnp.zeros_like(KM)

    for c in fetched[:4]:
        c.wait()
    rows[0:1, 0:96] = bond_v[...]
    rows[1:2, 0:96] = fresh_v[...]
    qb = rows[0:1, :]
    col_qb = column(qb)
    col_fresh = column(rows[1:2, :])
    fresh_half = jnp.where(sec == 0, col_fresh[0:48, :], col_fresh[48:96, :])
    left_diff = fresh_half[:, :96] - qb[:, :96]
    for l in range(6):
        for m in range(6):
            keep = left_diff == link_s[0, l] - link_s[0, m]
            LF[pl.ds((l * 6 + m) * 48, 48), 0:96] = jnp.where(keep, left_v[l, m].astype(F32), 0.0)

    pl.semaphore_wait(barrier, len(peers))

    def remote(src, dst, send, recv, peer):
        return pltpu.make_async_remote_copy(src_ref=src, dst_ref=dst, send_sem=send, recv_sem=recv,
                                            device_id=peer, device_id_type=MESH)

    charges = [remote(bond, bond_n, csend.at[0], crecv.at[0], before),
               remote(link, link_n, csend.at[1], crecv.at[1], before),
               remote(fresh, fresh_n, csend.at[2], crecv.at[2], before)]
    for c in charges:
        c.start()
    mps_send = remote(mps_h, MB.at[sec], msend, mrecv, partner)
    mps_send.start()
    right_send = remote(right_h, RB.at[sec], rsend, rrecv, before)
    right_send.start()
    right_forward = remote(RB.at[sec], RB.at[sec], fsend, frecv, partner)

    for i in range(48):
        L2F[i % 4, pl.ds(40 * (i // 4), 36), :] = LF[pl.ds(i, 36, stride=48), :]
    L2[...] = L2F[...].astype(BF16)
    W1[:, :, 240:256, :] = jnp.zeros((6, 6, 16, 768), BF16)
    for c in fetched[4:]:
        c.wait()
    KF[:, 0:6] = KH[...].astype(F32)
    ket = None
    for i in range(12):
        part = KF[pl.ds(i, 36, stride=12), :]
        part = part if i == 0 else pltpu.roll(part, 8 * i, axis=1)
        ket = part if ket is None else ket + part

    for c in charges:
        c.wait_recv()
    rows[2:3, 0:96] = bond_n[...]
    rows[3:4, 0:96] = fresh_n[...]
    rows[4:5, 0:6] = link_v[...]
    rows[5:6, 0:6] = link_n[...]
    rows[6:8, 0:6] = vert_v[0]
    qbn = rows[2:3, :]

    def operators():
        charge_rows = rows[...].astype(F32)
        ket_rows = jnp.sum(narrow[880:928, :].astype(F32) * charge_rows[6:7, :]
                           + narrow[928:976, :].astype(F32) * charge_rows[4:5, :], axis=1, keepdims=True)
        lower = jnp.broadcast_to(charge_rows[7:8, :], (16, 128)).astype(BF16)
        ahead = jnp.broadcast_to(charge_rows[5:6, :], (16, 128)).astype(BF16)
        ket_cols = (jnp.dot(lower, narrow[624:752, :], preferred_element_type=F32)
                    + jnp.dot(ahead, narrow[752:880, :], preferred_element_type=F32)
                    + narrow[976:992, :].astype(F32))[0:1, :]
        keep = jnp.abs(ket_rows[0:36] - ket_cols) < 0.5
        KM[0:36, :] = jnp.where(keep, ket, 0.0).astype(BF16)
        spread = lax.dot_general(narrow[0:432, :], KM[...], (((1,), (1,)), ((), ())), preferred_element_type=F32)
        KB2[...] = (jnp.dot(spread.astype(BF16), wide[0:48, :], preferred_element_type=F32)
                    * wide[48:480, :].astype(F32)).astype(BF16)
        total = None
        for p in range(2):
            spread = lax.dot_general(narrow[432 + 96 * p:528 + 96 * p, :], KM[...], (((1,), (1,)), ((), ())),
                                     preferred_element_type=F32)
            part = jnp.dot(spread.astype(BF16), wide[480 + 48 * p:528 + 48 * p, :], preferred_element_type=F32)
            total = part if total is None else total + part
        KB3[...] = (total * wide[576:672, :].astype(F32)).astype(BF16)

    operators()
    bond_diff = qbn[:, :96] - col_qb[:96, :96]
    mps_send.wait_recv()

    def boundary(i):
        up, vp = i // 3, i % 3
        for v in (2 * vp, 2 * vp + 1):
            for u in (2 * up, 2 * up + 1):
                keep = bond_diff == vert_s[0, 0, u] - vert_s[0, 0, v]
                t = jnp.concatenate([MB[0, u, v], MB[1, u, v]], axis=0).astype(F32)
                first, second = lane_parts(jnp.where(keep, t, 0.0))
                at = ((u % 2) + 2 * (v % 2)) * 128
                for k in range(3):
                    MS[i % 3, k, 0:96, at:at + 128] = first[k].astype(BF16)
                    MS[i % 3, k, 128:224, at:at + 128] = second[k].astype(BF16)

    def step1(i):
        up, vp = i // 3, i % 3
        for t in range(3):
            rhs = MS[i % 3, t]
            for c in range(480 // CHUNK1):
                lo = CHUNK1 * c
                lhs = jnp.concatenate([L2[t, lo:lo + CHUNK1, :], L2[t + 1, lo:lo + CHUNK1, :]], axis=1)
                o = jnp.dot(lhs, rhs, preferred_element_type=F32)
                for k in range(CHUNK1 // 40):
                    q = (CHUNK1 // 40) * c + k
                    for h in range(2):
                        w = jnp.concatenate([o[40 * k:40 * k + 40, 256 * h:256 * h + 128],
                                             o[40 * k:40 * k + 40, 256 * h + 128:256 * h + 256]], axis=0)
                        at = (q % 2) * 384 + t * 128
                        W1[q // 2, 2 * vp + h, up * 80:up * 80 + 80, at:at + 128] = w.astype(BF16)

    boundary(0)
    for i in range(9):
        if i < 8:
            boundary(i + 1)
        step1(i)

    def do2(qp):
        for vp in range(3):
            oa = jnp.dot(KB2[...], W1[qp, 2 * vp], preferred_element_type=F32)
            ob = jnp.dot(KB2[...], W1[qp, 2 * vp + 1], preferred_element_type=F32)
            for g in range(18):
                t = jnp.concatenate([oa[24 * g:24 * g + 24], ob[24 * g:24 * g + 24]], axis=0)
                W2[qp % 2, g, 48 * vp:48 * vp + 48, :] = t.astype(BF16)

    def do3(qp):
        for g in range(18):
            d, rp = g // 3, g % 3
            o = jnp.dot(KB3[:, 0:144], W2[qp % 2, g], preferred_element_type=F32)
            for i in range(12):
                at = ((2 * rp + i // 6) * 6 + i % 6) * 128
                row = qp * 96 + d * 16
                for t in range(3):
                    w = jnp.concatenate([o[8 * i:8 * i + 8, 128 * t:128 * t + 128],
                                         o[8 * i:8 * i + 8, 384 + 128 * t:512 + 128 * t]], axis=0)
                    W3[t, row:row + 16, at:at + 128] = w.astype(BF16)

    def right(r_range):
        right_diff = column(rows[3:4, :])[:96, :96] - qbn[:, :96]
        ahead_row = rows[5:6, :]
        for r in r_range:
            for s in range(6):
                keep = right_diff == ahead_row[:, r:r + 1] - ahead_row[:, s:s + 1]
                t = jnp.concatenate([RB[0, r, s], RB[1, r, s]], axis=0).astype(F32)
                first, second = lane_parts(jnp.where(keep, t, 0.0))
                at = (r * 6 + s) * 128
                for k in range(3):
                    RS[k, 0:96, at:at + 128] = first[k].astype(BF16)
                    RS[k, 128:224, at:at + 128] = second[k].astype(BF16)

    do2(0)
    for qp in range(1, 6):
        if qp == FORWARD_AT:
            right_send.wait_recv()
            right_forward.start()
        if qp == FORWARD_AT + 1:
            right_forward.wait_recv()
            right(range(0, 3))
        if qp == FORWARD_AT + 2:
            right(range(3, 6))
        do2(qp)
        do3(qp - 1)
    do3(5)

    for t in range(3):
        O4[t] = lax.dot_general(W3[t], RS[t], (((1,), (1,)), ((), ())), preferred_element_type=F32)
    acc = jnp.zeros((8, 96), F32)
    for qp in range(6):
        for d in range(6):
            for h in range(2):
                row = qp * 96 + d * 16 + h * 8
                o = [O4[t, row:row + 8, :] for t in range(3)]
                parts = [o[0][:, 0:96], o[0][:, 128:224] + o[1][:, 0:96],
                         o[1][:, 128:224] + o[2][:, 0:96], o[2][:, 128:224]]
                for k in range(4):
                    at = (8 * qp + 4 * h + k) * 48 + d * 8
                    IMG[at:at + 8, 0:96] = parts[k]
                    acc = acc + parts[k] * parts[k]
    mine = jnp.sum(jnp.sum(acc, axis=0, keepdims=True), axis=1, keepdims=True)
    own = SA.at[sec, pl.ds(plane, 1), :]
    own[...] = jnp.broadcast_to(mine, (1, 128))
    plane_sends = [remote(own, own, asend.at[2 * k + f], arecv.at[2 * k + f], plane_peer(k, f))
                   for k in range(plane_n) for f in range(2) if k + f > 0]
    for c in plane_sends:
        c.start()
    plane_sends[0].wait_recv()

    meansq = (SA[0, pl.ds(plane, 1), :] + SA[1, pl.ds(plane, 1), :]) / 331776.0
    scale = lax.rsqrt(meansq + 1e-06)
    for d in range(6):
        for e in range(6):
            t = IMG[pl.ds(d * 8 + e, 48, stride=48), 0:96]
            OUT[d, e] = (t * scale[:, 0:96]).astype(BF16)
    out_copy = pltpu.make_async_copy(OUT, out_h, osem)
    out_copy.start()

    for c in plane_sends[1:]:
        c.wait_recv()
    logs = 0.5 * jnp.log((SA[0] + SA[1]) / 331776.0 + 1e-06)
    SB[pl.ds(z, 1), :] = jnp.sum(logs, axis=0, keepdims=True)
    line = SB.at[pl.ds(z, 1), :]
    line_sends = [remote(line, line, bsend.at[k], brecv.at[k], line_peer(k)) for k in range(1, nz)]
    for c in line_sends:
        c.start()
    for c in line_sends:
        c.wait_recv()
    log_out[...] = jnp.sum(SB[...], axis=0, keepdims=True) / float(count)

    for c in charges + [mps_send, right_send, right_forward] + plane_sends + line_sends:
        c.wait_send()
    out_copy.wait()


def local(sizes, mps, ket, left_proj, right_proj, bond_charge, new_charge, link_charge, vert_charge):
    nx, nz, ny, _ = sizes
    mps_v = mps[0].transpose(1, 2, 0, 3)
    left_v = left_proj[0].transpose(2, 3, 0, 1)
    right_v = right_proj[0].transpose(1, 2, 3, 0)
    ket_v = ket.transpose(0, 1, 2, 3, 5, 4).reshape(432, 6)
    vm = pl.BlockSpec(memory_space=pltpu.VMEM)
    hbm = pl.BlockSpec(memory_space=pl.ANY)
    dma = pltpu.SemaphoreType.DMA
    out, log_row = pl.pallas_call(
        lambda *refs: kernel(sizes, *refs),
        out_shape=(jax.ShapeDtypeStruct((6, 6, 48, 96), BF16), jax.ShapeDtypeStruct((1, 128), F32)),
        in_specs=[hbm] * 10,
        out_specs=(hbm, vm),
        scratch_shapes=[
            pltpu.VMEM((8, 128), I32),
            pltpu.VMEM((1, 96), I32), pltpu.VMEM((1, 96), I32), pltpu.VMEM((1, 6), I32), pltpu.VMEM((1, 2, 6), I32),
            pltpu.VMEM((1, 96), I32), pltpu.VMEM((1, 96), I32), pltpu.VMEM((1, 6), I32),
            pltpu.SMEM((1, 6), I32), pltpu.SMEM((1, 2, 6), I32),
            pltpu.VMEM((992, 128), BF16), pltpu.VMEM((672, 256), BF16),
            pltpu.VMEM((432, 6), BF16), pltpu.VMEM((432, 128), F32),
            pltpu.VMEM((6, 6, 48, 96), BF16),
            pltpu.VMEM((2, 6, 6, 48, 96), BF16), pltpu.VMEM((2, 6, 6, 48, 96), BF16),
            pltpu.VMEM((1728, 128), F32), pltpu.VMEM((4, 480, 128), F32), pltpu.VMEM((4, 480, 128), BF16),
            pltpu.VMEM((3, 3, 256, 512), BF16), pltpu.VMEM((3, 256, 4608), BF16),
            pltpu.VMEM((48, 128), BF16), pltpu.VMEM((432, 256), BF16), pltpu.VMEM((96, 256), BF16),
            pltpu.VMEM((6, 6, 256, 768), BF16), pltpu.VMEM((2, 18, 144, 768), BF16),
            pltpu.VMEM((3, 576, 4608), BF16), pltpu.VMEM((3, 576, 256), F32), pltpu.VMEM((2304, 128), F32),
            pltpu.VMEM((6, 6, 48, 96), BF16),
            pltpu.VMEM((2, nx * ny, 128), F32), pltpu.VMEM((nz, 128), F32),
            dma((11,)), dma((3,)), dma((3,)), dma(()), dma(()), dma(()), dma(()), dma(()), dma(()),
            dma((2 * nx * ny,)), dma((2 * nx * ny,)), dma((nz,)), dma((nz,)), dma(())],
        compiler_params=pltpu.CompilerParams(
            vmem_limit_bytes=VMEM_LIMIT, collective_id=0, has_side_effects=True),
    )(bond_charge, new_charge, link_charge, vert_charge, *operator_tables(), ket_v, mps_v, left_v, right_v)
    return out.transpose(2, 0, 1, 3)[None], log_row[0, 0]


def solution(mesh):
    if mesh.shape["col"] == 128:
        sizes = (4, 8, 4, mesh.shape["sec"])
    else:
        sizes = (2, mesh.shape["col"] // 4, 2, mesh.shape["sec"])
    torus = Mesh(mesh.devices.reshape(sizes), (*COL, "sec"))
    in_specs = (
        P(COL, "sec", None, None, None),
        P(COL, None, None, None, None, None),
        P(COL, "sec", None, None, None),
        P(COL, None, None, None, "sec"),
        P(COL, None),
        P(COL, None),
        P(COL, None),
        P(COL, None, None),
    )
    out_specs = (P(COL, "sec", None, None, None), P())
    return jax.shard_map(lambda *a: local(sizes, *a), mesh=torus, in_specs=in_specs, out_specs=out_specs,
                         check_vma=False)
```

time: 70 us -> 49.7 us (0.71)
  Pallas kernels: 62.9 us -> 45.6 us
  local copies, waits for them, and re-layouts: 4.3 us -> 1.81 us
    pallas_call x1, Pallas kernels: 62.9 us -> 45.6 us  [local(): pl.pallas_call(lambda *refs: kernel(sizes, *refs), out_shape=(jax.ShapeDt...]
    unnamed x4 -> x3, local copies, waits for them, and re-layouts: 3.46 us -> 1.81 us
    reshape x2 -> x0, local copies, waits for them, and re-layouts: 0.84 us -> none  [local(): ketm = ket.reshape(36, 72)]
where the time goes in v2:
time: 49.7 us; the launch traced here: 49.2 us
  Pallas kernels  45.6 us (92%)
  between operations  1.82 us (4%)
  local copies, waits for them, and re-layouts  1.81 us (4%)
    pallas_call x1, Pallas kernels, local(): pl.pallas_call(lambda *refs: kernel(sizes, *refs), out_shape=(jax.ShapeDt...  45.6 us
    unnamed x3, local copies, waits for them, and re-layouts  1.81 us

profile of v2, /device:TPU:32, one launch (start us, length us, event | category | flops | bytes accessed | tf_op | source)
XLA Modules:
  0.0 49.2 jit_solution(6408314992704418510)
XLA Ops:
  0.6 45.6 %shard_map.113 = (bf16[6,6,48,96]{3,2,1,0:T(8,128)(2,1)}, f32[1,128]{1,0:T(1,128)}) custom-call(s32[1,96]{1,0:T(1,128)} %refs_0_.1, s32[1,96]{1,0:T(1,128)} %refs_1_.1, s32[1,6]{1,0:T(1,128)} %refs_2_.1, s32[1,2,6]{2,1,0:T(2,128)} %refs_3_.1, bf16[992,128]{1,0:T(8,128)(2,1)} %constant.4.clone.refs_4_, bf16[672,256]{1,0:T(8,128)(2,1)} %constant.5.clone.refs_5_, ...), custom_call_target="tpu_custom_call" | custom-call | tf_op jit(solution)/shard_map/pallas_call | solution.py:351
  46.2 0.0 copy-start
  46.2 1.8 %copy.14 = bf16[1,48,6,6,96]{4,1,3,2,0:T(8,128)(2,1)} copy(bf16[1,48,6,6,96]{4,1,3,2,0:T(8,128)(2,1)} %bitcast.17) | data formatting | bytes 663552
  48.0 0.0 copy-done
Async XLA Ops:
  46.2 1.8 %copy-start = (f32[1,128]{1,0:T(1,128)S(1)}, f32[1,128]{1,0:T(1,128)}, u32[]{:S(2)}) copy-start(f32[1,128]{1,0:T(1,128)} %get-tuple-element.5) | copy-start | bytes 1540

commit v3 on v2

--- a/solution.py
+++ b/solution.py
@@ -11,7 +11,7 @@
 COL = ("col_0", "col_1", "col_2")
 F32, BF16, I32 = jnp.float32, jnp.bfloat16, jnp.int32
 MESH = pl.DeviceIdType.MESH
-FORWARD_AT = 3
+FORWARD_AT = 4
 CHUNK1 = 480
 VMEM_LIMIT = 67_043_328
 
@@ -32,7 +32,7 @@
                 hr[r, lane] = 1
                 hp[:, lane] = p
                 for m in range(6):
-                    row = ((d * 6 + r) * 6 + m) * 2 + p
+                    row = ((r * 6 + d) * 6 + m) * 2 + p
                     e2[row, lane] = 1
                     rows_m[row] = m
     gu = np.zeros((48, 128), np.float32)
@@ -45,25 +45,25 @@
                 f2[u * 6 + l, u * 40 + l * 6 + m] = 1
                 cols_m[u * 40 + l * 6 + m] = m
     k2 = rows_m[:, None] == cols_m[None, :]
-    e3 = np.zeros((2, 96, 128), np.float32)
+    e3 = np.zeros((2, 80, 128), np.float32)
     f3 = np.zeros((2, 48, 256), np.float32)
-    rows_r = np.full(96, -1)
-    cols_r = np.full(256, -2)
-    for r in range(2):
+    rows_d = np.full(80, -1)
+    cols_d = np.full(256, -2)
+    for d in range(2):
         for s in range(6):
             for e in range(6):
-                row = (r * 6 + s) * 8 + e
-                rows_r[row] = r
+                row = (s * 2 + d) * 6 + e
+                rows_d[row] = d
                 for p in range(2):
                     e3[p, row, (2 * e + p) * 8 + s] = 1
         for v in range(6):
             for m in range(6):
                 for p in range(2):
-                    col = v * 24 + r * 12 + m * 2 + p
-                    cols_r[col] = r
+                    col = v * 24 + d * 12 + m * 2 + p
+                    cols_d[col] = d
                     f3[p, v * 6 + m, col] = 1
-    k3 = rows_r[:, None] == cols_r[None, :]
-    narrow = np.concatenate([e2, e3.reshape(192, 128), hd, hr, gu, gl, hp])
+    k3 = rows_d[:, None] == cols_d[None, :]
+    narrow = np.concatenate([e2, e3.reshape(160, 128), hd, hr, gu, gl, hp])
     wide = np.concatenate([f2, k2, f3.reshape(96, 256), k3])
     return jnp.asarray(narrow, BF16), jnp.asarray(wide, BF16)
 
@@ -100,25 +100,27 @@
     after = place(lax.rem(site + 1, count))
     partner = {"sec": other}
     plane = x * ny + y
-    plane_n = nx * ny
-
-    def plane_peer(k, flip):
-        q = lax.rem(plane + k, plane_n)
-        return {"col_0": lax.div(q, ny), "col_2": lax.rem(q, ny), "sec": other if flip else sec}
+
+    def plane_peer(dx, dy, flip):
+        return {"col_0": lax.rem(x + dx, nx), "col_2": lax.rem(y + dy, ny), "sec": other if flip else sec}
+
+    offsets = [(dx, dy, f) for dx in range(nx) for dy in range(ny) for f in range(2) if dx + dy + f > 0]
+    offsets.sort(key=lambda o: -min(o[0], nx - o[0]) - min(o[1], ny - o[1]))
+    offsets.remove((0, 0, 1))
+    offsets = [(0, 0, 1)] + offsets
+    line_offsets = sorted(range(1, nz), key=lambda k: -min(k, nz - k))
 
     def line_peer(k):
         return {"col_1": lax.rem(z + k, nz)}
 
     barrier = pltpu.get_barrier_semaphore()
-    peers = [before, after]
-    peers += [plane_peer(k, f) for k in range(plane_n) for f in range(2) if k + f > 0]
-    peers += [line_peer(k) for k in range(1, nz)]
+    peers = [line_peer(k) for k in line_offsets] + [plane_peer(*o) for o in offsets] + [before, after]
     for peer in peers:
         pl.semaphore_signal(barrier, inc=1, device_id=peer, device_id_type=MESH)
 
     fetched = [pltpu.make_async_copy(src, dst, lsem.at[i]) for i, (src, dst) in enumerate([
-        (link, link_s), (bond, bond_v), (fresh, fresh_v), (left_h, left_v), (vert, vert_s), (link, link_v),
-        (vert, vert_v), (ket_h, KH), (narrow_h, narrow), (wide_h, wide), (mps_h, MB.at[sec])])]
+        (link, link_s), (bond, bond_v), (fresh, fresh_v), (left_h, left_v), (link, link_v), (mps_h, MB.at[sec]),
+        (vert, vert_s), (vert, vert_v), (ket_h, KH), (narrow_h, narrow), (wide_h, wide)])]
     for c in fetched:
         c.start()
 
@@ -144,18 +146,20 @@
             keep = left_diff == link_s[0, l] - link_s[0, m]
             LF[pl.ds((l * 6 + m) * 48, 48), 0:96] = jnp.where(keep, left_v[l, m].astype(F32), 0.0)
 
+    for c in fetched[4:6]:
+        c.wait()
     pl.semaphore_wait(barrier, len(peers))
 
     def remote(src, dst, send, recv, peer):
         return pltpu.make_async_remote_copy(src_ref=src, dst_ref=dst, send_sem=send, recv_sem=recv,
                                             device_id=peer, device_id_type=MESH)
 
-    charges = [remote(bond, bond_n, csend.at[0], crecv.at[0], before),
-               remote(link, link_n, csend.at[1], crecv.at[1], before),
-               remote(fresh, fresh_n, csend.at[2], crecv.at[2], before)]
+    charges = [remote(bond_v, bond_n, csend.at[0], crecv.at[0], before),
+               remote(link_v, link_n, csend.at[1], crecv.at[1], before),
+               remote(fresh_v, fresh_n, csend.at[2], crecv.at[2], before)]
     for c in charges:
         c.start()
-    mps_send = remote(mps_h, MB.at[sec], msend, mrecv, partner)
+    mps_send = remote(MB.at[sec], MB.at[sec], msend, mrecv, partner)
     mps_send.start()
     right_send = remote(right_h, RB.at[sec], rsend, rrecv, before)
     right_send.start()
@@ -165,7 +169,7 @@
         L2F[i % 4, pl.ds(40 * (i // 4), 36), :] = LF[pl.ds(i, 36, stride=48), :]
     L2[...] = L2F[...].astype(BF16)
     W1[:, :, 240:256, :] = jnp.zeros((6, 6, 16, 768), BF16)
-    for c in fetched[4:]:
+    for c in fetched[6:]:
         c.wait()
     KF[:, 0:6] = KH[...].astype(F32)
     ket = None
@@ -185,13 +189,13 @@
 
     def operators():
         charge_rows = rows[...].astype(F32)
-        ket_rows = jnp.sum(narrow[880:928, :].astype(F32) * charge_rows[6:7, :]
-                           + narrow[928:976, :].astype(F32) * charge_rows[4:5, :], axis=1, keepdims=True)
+        ket_rows = jnp.sum(narrow[848:896, :].astype(F32) * charge_rows[6:7, :]
+                           + narrow[896:944, :].astype(F32) * charge_rows[4:5, :], axis=1, keepdims=True)
         lower = jnp.broadcast_to(charge_rows[7:8, :], (16, 128)).astype(BF16)
         ahead = jnp.broadcast_to(charge_rows[5:6, :], (16, 128)).astype(BF16)
-        ket_cols = (jnp.dot(lower, narrow[624:752, :], preferred_element_type=F32)
-                    + jnp.dot(ahead, narrow[752:880, :], preferred_element_type=F32)
-                    + narrow[976:992, :].astype(F32))[0:1, :]
+        ket_cols = (jnp.dot(lower, narrow[592:720, :], preferred_element_type=F32)
+                    + jnp.dot(ahead, narrow[720:848, :], preferred_element_type=F32)
+                    + narrow[944:960, :].astype(F32))[0:1, :]
         keep = jnp.abs(ket_rows[0:36] - ket_cols) < 0.5
         KM[0:36, :] = jnp.where(keep, ket, 0.0).astype(BF16)
         spread = lax.dot_general(narrow[0:432, :], KM[...], (((1,), (1,)), ((), ())), preferred_element_type=F32)
@@ -199,13 +203,12 @@
                     * wide[48:480, :].astype(F32)).astype(BF16)
         total = None
         for p in range(2):
-            spread = lax.dot_general(narrow[432 + 96 * p:528 + 96 * p, :], KM[...], (((1,), (1,)), ((), ())),
+            spread = lax.dot_general(narrow[432 + 80 * p:512 + 80 * p, :], KM[...], (((1,), (1,)), ((), ())),
                                      preferred_element_type=F32)
             part = jnp.dot(spread.astype(BF16), wide[480 + 48 * p:528 + 48 * p, :], preferred_element_type=F32)
             total = part if total is None else total + part
-        KB3[...] = (total * wide[576:672, :].astype(F32)).astype(BF16)
-
-    operators()
+        KB3[...] = (total * wide[576:656, :].astype(F32)).astype(BF16)
+
     bond_diff = qbn[:, :96] - col_qb[:96, :96]
     mps_send.wait_recv()
 
@@ -238,6 +241,7 @@
                         W1[q // 2, 2 * vp + h, up * 80:up * 80 + 80, at:at + 128] = w.astype(BF16)
 
     boundary(0)
+    operators()
     for i in range(9):
         if i < 8:
             boundary(i + 1)
@@ -253,15 +257,15 @@
 
     def do3(qp):
         for g in range(18):
-            d, rp = g // 3, g % 3
-            o = jnp.dot(KB3[:, 0:144], W2[qp % 2, g], preferred_element_type=F32)
-            for i in range(12):
-                at = ((2 * rp + i // 6) * 6 + i % 6) * 128
-                row = qp * 96 + d * 16
+            r, dp = g // 3, g % 3
+            o = jnp.dot(KB3[0:72, 0:144], W2[qp % 2, g], preferred_element_type=F32)
+            row = qp * 72 + dp * 24
+            for i in range(6):
+                at = (r * 6 + i) * 128
                 for t in range(3):
-                    w = jnp.concatenate([o[8 * i:8 * i + 8, 128 * t:128 * t + 128],
-                                         o[8 * i:8 * i + 8, 384 + 128 * t:512 + 128 * t]], axis=0)
-                    W3[t, row:row + 16, at:at + 128] = w.astype(BF16)
+                    w = jnp.concatenate([o[12 * i:12 * i + 12, 128 * t:128 * t + 128],
+                                         o[12 * i:12 * i + 12, 384 + 128 * t:512 + 128 * t]], axis=0)
+                    W3[t, row:row + 24, at:at + 128] = w.astype(BF16)
 
     def right(r_range):
         right_diff = column(rows[3:4, :])[:96, :96] - qbn[:, :96]
@@ -281,34 +285,33 @@
         if qp == FORWARD_AT:
             right_send.wait_recv()
             right_forward.start()
-        if qp == FORWARD_AT + 1:
-            right_forward.wait_recv()
-            right(range(0, 3))
-        if qp == FORWARD_AT + 2:
-            right(range(3, 6))
         do2(qp)
         do3(qp - 1)
+    right_forward.wait_recv()
+    right(range(6))
     do3(5)
 
     for t in range(3):
         O4[t] = lax.dot_general(W3[t], RS[t], (((1,), (1,)), ((), ())), preferred_element_type=F32)
-    acc = jnp.zeros((8, 96), F32)
+    acc = jnp.zeros((12, 96), F32)
     for qp in range(6):
-        for d in range(6):
+        for dp in range(3):
             for h in range(2):
-                row = qp * 96 + d * 16 + h * 8
-                o = [O4[t, row:row + 8, :] for t in range(3)]
+                row = qp * 72 + dp * 24 + h * 12
+                o = [O4[t, row:row + 12, :] for t in range(3)]
                 parts = [o[0][:, 0:96], o[0][:, 128:224] + o[1][:, 0:96],
                          o[1][:, 128:224] + o[2][:, 0:96], o[2][:, 128:224]]
                 for k in range(4):
-                    at = (8 * qp + 4 * h + k) * 48 + d * 8
-                    IMG[at:at + 8, 0:96] = parts[k]
+                    at = (8 * qp + 4 * h + k) * 36 + dp * 12
+                    IMG[at:at + 12, 0:96] = parts[k]
                     acc = acc + parts[k] * parts[k]
     mine = jnp.sum(jnp.sum(acc, axis=0, keepdims=True), axis=1, keepdims=True)
     own = SA.at[sec, pl.ds(plane, 1), :]
     own[...] = jnp.broadcast_to(mine, (1, 128))
-    plane_sends = [remote(own, own, asend.at[2 * k + f], arecv.at[2 * k + f], plane_peer(k, f))
-                   for k in range(plane_n) for f in range(2) if k + f > 0]
+    plane_sends = []
+    for dx, dy, f in offsets:
+        i = 2 * (dx * ny + dy) + f
+        plane_sends.append(remote(own, own, asend.at[i], arecv.at[i], plane_peer(dx, dy, f)))
     for c in plane_sends:
         c.start()
     plane_sends[0].wait_recv()
@@ -317,7 +320,7 @@
     scale = lax.rsqrt(meansq + 1e-06)
     for d in range(6):
         for e in range(6):
-            t = IMG[pl.ds(d * 8 + e, 48, stride=48), 0:96]
+            t = IMG[pl.ds(d * 6 + e, 48, stride=36), 0:96]
             OUT[d, e] = (t * scale[:, 0:96]).astype(BF16)
     out_copy = pltpu.make_async_copy(OUT, out_h, osem)
     out_copy.start()
@@ -327,7 +330,7 @@
     logs = 0.5 * jnp.log((SA[0] + SA[1]) / 331776.0 + 1e-06)
     SB[pl.ds(z, 1), :] = jnp.sum(logs, axis=0, keepdims=True)
     line = SB.at[pl.ds(z, 1), :]
-    line_sends = [remote(line, line, bsend.at[k], brecv.at[k], line_peer(k)) for k in range(1, nz)]
+    line_sends = [remote(line, line, bsend.at[k], brecv.at[k], line_peer(k)) for k in line_offsets]
     for c in line_sends:
         c.start()
     for c in line_sends:
@@ -358,15 +361,15 @@
             pltpu.VMEM((1, 96), I32), pltpu.VMEM((1, 96), I32), pltpu.VMEM((1, 6), I32), pltpu.VMEM((1, 2, 6), I32),
             pltpu.VMEM((1, 96), I32), pltpu.VMEM((1, 96), I32), pltpu.VMEM((1, 6), I32),
             pltpu.SMEM((1, 6), I32), pltpu.SMEM((1, 2, 6), I32),
-            pltpu.VMEM((992, 128), BF16), pltpu.VMEM((672, 256), BF16),
+            pltpu.VMEM((960, 128), BF16), pltpu.VMEM((656, 256), BF16),
             pltpu.VMEM((432, 6), BF16), pltpu.VMEM((432, 128), F32),
             pltpu.VMEM((6, 6, 48, 96), BF16),
             pltpu.VMEM((2, 6, 6, 48, 96), BF16), pltpu.VMEM((2, 6, 6, 48, 96), BF16),
             pltpu.VMEM((1728, 128), F32), pltpu.VMEM((4, 480, 128), F32), pltpu.VMEM((4, 480, 128), BF16),
             pltpu.VMEM((3, 3, 256, 512), BF16), pltpu.VMEM((3, 256, 4608), BF16),
-            pltpu.VMEM((48, 128), BF16), pltpu.VMEM((432, 256), BF16), pltpu.VMEM((96, 256), BF16),
+            pltpu.VMEM((48, 128), BF16), pltpu.VMEM((432, 256), BF16), pltpu.VMEM((80, 256), BF16),
             pltpu.VMEM((6, 6, 256, 768), BF16), pltpu.VMEM((2, 18, 144, 768), BF16),
-            pltpu.VMEM((3, 576, 4608), BF16), pltpu.VMEM((3, 576, 256), F32), pltpu.VMEM((2304, 128), F32),
+            pltpu.VMEM((3, 432, 4608), BF16), pltpu.VMEM((3, 432, 256), F32), pltpu.VMEM((1728, 128), F32),
             pltpu.VMEM((6, 6, 48, 96), BF16),
             pltpu.VMEM((2, nx * ny, 128), F32), pltpu.VMEM((nz, 128), F32),
             dma((11,)), dma((3,)), dma((3,)), dma(()), dma(()), dma(()), dma(()), dma(()), dma(()),

time: 49.7 us -> 49.4 us (level)
  no operation moved by 1% of the time
where the time goes in v3:
time: 49.4 us; the launch traced here: 48.9 us
  Pallas kernels  45.3 us (92%)
  between operations  1.82 us (4%)
  local copies, waits for them, and re-layouts  1.81 us (4%)
    pallas_call x1, Pallas kernels, local(): pl.pallas_call(lambda *refs: kernel(sizes, *refs), out_shape=(jax.ShapeDt...  45.3 us
    unnamed x3, local copies, waits for them, and re-layouts  1.81 us

profile of v3, /device:TPU:32, one launch (start us, length us, event | category | flops | bytes accessed | tf_op | source)
XLA Modules:
  0.0 48.9 jit_solution(10288509930902723534)
XLA Ops:
  0.6 45.3 %shard_map.113 = (bf16[6,6,48,96]{3,2,1,0:T(8,128)(2,1)}, f32[1,128]{1,0:T(1,128)}) custom-call(s32[1,96]{1,0:T(1,128)} %refs_0_.1, s32[1,96]{1,0:T(1,128)} %refs_1_.1, s32[1,6]{1,0:T(1,128)} %refs_2_.1, s32[1,2,6]{2,1,0:T(2,128)} %refs_3_.1, bf16[960,128]{1,0:T(8,128)(2,1)} %constant.4.clone.refs_4_, bf16[656,256]{1,0:T(8,128)(2,1)} %constant.5.clone.refs_5_, ...), custom_call_target="tpu_custom_call" | custom-call | tf_op jit(solution)/shard_map/pallas_call | solution.py:354
  45.9 0.0 copy-start
  45.9 1.8 %copy.14 = bf16[1,48,6,6,96]{4,1,3,2,0:T(8,128)(2,1)} copy(bf16[1,48,6,6,96]{4,1,3,2,0:T(8,128)(2,1)} %bitcast.17) | data formatting | bytes 663552
  47.7 0.0 copy-done
Async XLA Ops:
  45.9 1.8 %copy-start = (f32[1,128]{1,0:T(1,128)S(1)}, f32[1,128]{1,0:T(1,128)}, u32[]{:S(2)}) copy-start(f32[1,128]{1,0:T(1,128)} %get-tuple-element.5) | copy-start | bytes 1540

commit v4 on v3

--- a/solution.py
+++ b/solution.py
@@ -13,7 +13,7 @@
 MESH = pl.DeviceIdType.MESH
 FORWARD_AT = 4
 CHUNK1 = 480
-VMEM_LIMIT = 67_043_328
+VMEM_LIMIT = 60_000_000
 
 
 def operator_tables():
@@ -83,9 +83,9 @@
 
 def kernel(sizes, bond, fresh, link, vert, narrow_h, wide_h, ket_h, mps_h, left_h, right_h, out_h, log_out,
            rows, bond_v, fresh_v, link_v, vert_v, bond_n, fresh_n, link_n, link_s, vert_s,
-           narrow, wide, KH, KF, left_v, MB, RB, LF, L2F, L2, MS, RS, KM, KB2, KB3, W1, W2, W3, O4, IMG, OUT,
+           narrow, wide, KH, KF, left_v, MB, RB, LF, L2F, L2, MS, RS, KM, KB2, KB3, W1, W2, W3, O4, IMG,
            SA, SB,
-           lsem, csend, crecv, msend, mrecv, rsend, rrecv, fsend, frecv, asend, arecv, bsend, brecv, osem):
+           lsem, csend, crecv, msend, mrecv, rsend, rrecv, fsend, frecv, asend, arecv, bsend, brecv):
     nx, nz, ny, _ = sizes
     x, z, y = lax.axis_index("col_0"), lax.axis_index("col_1"), lax.axis_index("col_2")
     sec = lax.axis_index("sec")
@@ -321,9 +321,7 @@
     for d in range(6):
         for e in range(6):
             t = IMG[pl.ds(d * 6 + e, 48, stride=36), 0:96]
-            OUT[d, e] = (t * scale[:, 0:96]).astype(BF16)
-    out_copy = pltpu.make_async_copy(OUT, out_h, osem)
-    out_copy.start()
+            out_h[d, e] = (t * scale[:, 0:96]).astype(BF16)
 
     for c in plane_sends[1:]:
         c.wait_recv()
@@ -339,7 +337,6 @@
 
     for c in charges + [mps_send, right_send, right_forward] + plane_sends + line_sends:
         c.wait_send()
-    out_copy.wait()
 
 
 def local(sizes, mps, ket, left_proj, right_proj, bond_charge, new_charge, link_charge, vert_charge):
@@ -353,9 +350,9 @@
     dma = pltpu.SemaphoreType.DMA
     out, log_row = pl.pallas_call(
         lambda *refs: kernel(sizes, *refs),
-        out_shape=(jax.ShapeDtypeStruct((6, 6, 48, 96), BF16), jax.ShapeDtypeStruct((1, 128), F32)),
+        out_shape=(pltpu.VMEM((6, 6, 48, 96), BF16), jax.ShapeDtypeStruct((1, 128), F32)),
         in_specs=[hbm] * 10,
-        out_specs=(hbm, vm),
+        out_specs=(vm, vm),
         scratch_shapes=[
             pltpu.VMEM((8, 128), I32),
             pltpu.VMEM((1, 96), I32), pltpu.VMEM((1, 96), I32), pltpu.VMEM((1, 6), I32), pltpu.VMEM((1, 2, 6), I32),
@@ -370,10 +367,9 @@
             pltpu.VMEM((48, 128), BF16), pltpu.VMEM((432, 256), BF16), pltpu.VMEM((80, 256), BF16),
             pltpu.VMEM((6, 6, 256, 768), BF16), pltpu.VMEM((2, 18, 144, 768), BF16),
             pltpu.VMEM((3, 432, 4608), BF16), pltpu.VMEM((3, 432, 256), F32), pltpu.VMEM((1728, 128), F32),
-            pltpu.VMEM((6, 6, 48, 96), BF16),
             pltpu.VMEM((2, nx * ny, 128), F32), pltpu.VMEM((nz, 128), F32),
             dma((11,)), dma((3,)), dma((3,)), dma(()), dma(()), dma(()), dma(()), dma(()), dma(()),
-            dma((2 * nx * ny,)), dma((2 * nx * ny,)), dma((nz,)), dma((nz,)), dma(())],
+            dma((2 * nx * ny,)), dma((2 * nx * ny,)), dma((nz,)), dma((nz,))],
         compiler_params=pltpu.CompilerParams(
             vmem_limit_bytes=VMEM_LIMIT, collective_id=0, has_side_effects=True),
     )(bond_charge, new_charge, link_charge, vert_charge, *operator_tables(), ket_v, mps_v, left_v, right_v)

time: 49.4 us -> 48.3 us (0.978)
  local copies, waits for them, and re-layouts: 1.81 us -> 0.77 us
    unnamed x3, local copies, waits for them, and re-layouts: 1.81 us -> 0.77 us
where the time goes in v4:
time: 48.3 us; the launch traced here: 47.8 us
  Pallas kernels  45.2 us (94%)
  between operations  1.82 us (4%)
  local copies, waits for them, and re-layouts  0.77 us (2%)
    pallas_call x1, Pallas kernels, local(): pl.pallas_call(lambda *refs: kernel(sizes, *refs), out_shape=(pltpu.VMEM(...  45.2 us

profile of v4, /device:TPU:32, one launch (start us, length us, event | category | flops | bytes accessed | tf_op | source)
XLA Modules:
  0.0 47.8 jit_solution(13843496100780947408)
XLA Ops:
  0.6 45.2 %shard_map.113 = (bf16[6,6,48,96]{3,2,1,0:T(8,128)(2,1)S(1)}, f32[1,128]{1,0:T(1,128)}) custom-call(s32[1,96]{1,0:T(1,128)} %refs_0_.1, s32[1,96]{1,0:T(1,128)} %refs_1_.1, s32[1,6]{1,0:T(1,128)} %refs_2_.1, s32[1,2,6]{2,1,0:T(2,128)} %refs_3_.1, bf16[960,128]{1,0:T(8,128)(2,1)} %constant.4.clone.refs_4_, bf16[656,256]{1,0:T(8,128)(2,1)} %constant.5.clone.refs_5_, ...), custom_call_target="tpu_custom_call" | custom-call | tf_op jit(solution)/shard_map/pallas_call | solution.py:351
  45.8 0.0 copy-start
  45.8 0.8 %copy.14 = bf16[1,48,6,6,96]{4,1,3,2,0:T(8,128)(2,1)} copy(bf16[1,48,6,6,96]{4,1,3,2,0:T(8,128)(2,1)S(1)} %bitcast.17) | data formatting | bytes 663552
  46.6 0.0 copy-done
Async XLA Ops:
  45.8 0.8 %copy-start = (f32[1,128]{1,0:T(1,128)S(1)}, f32[1,128]{1,0:T(1,128)}, u32[]{:S(2)}) copy-start(f32[1,128]{1,0:T(1,128)} %get-tuple-element.5) | copy-start | bytes 1540

commit v5 on v4

--- a/solution.py
+++ b/solution.py
@@ -350,7 +350,7 @@
     dma = pltpu.SemaphoreType.DMA
     out, log_row = pl.pallas_call(
         lambda *refs: kernel(sizes, *refs),
-        out_shape=(pltpu.VMEM((6, 6, 48, 96), BF16), jax.ShapeDtypeStruct((1, 128), F32)),
+        out_shape=(pltpu.VMEM((6, 6, 48, 96), BF16), pltpu.VMEM((1, 128), F32)),
         in_specs=[hbm] * 10,
         out_specs=(vm, vm),
         scratch_shapes=[

time: 48.3 us -> 47.7 us (0.988)
  Pallas kernels: 45.2 us -> 44.6 us
    pallas_call x1, Pallas kernels: 45.2 us -> 44.6 us  [local(): pl.pallas_call(lambda *refs: kernel(sizes, *refs), out_shape=(pltpu.VMEM(...]
where the time goes in v5:
time: 47.7 us; the launch traced here: 47.2 us
  Pallas kernels  44.6 us (94%)
  between operations  1.81 us (4%)
  local copies, waits for them, and re-layouts  0.76 us (2%)
    pallas_call x1, Pallas kernels, local(): pl.pallas_call(lambda *refs: kernel(sizes, *refs), out_shape=(pltpu.VMEM(...  44.6 us

profile of v5, /device:TPU:32, one launch (start us, length us, event | category | flops | bytes accessed | tf_op | source)
XLA Modules:
  0.0 47.2 jit_solution(1780047657081123388)
XLA Ops:
  0.6 44.6 %shard_map.113 = (bf16[6,6,48,96]{3,2,1,0:T(8,128)(2,1)S(1)}, f32[1,128]{1,0:T(1,128)S(1)}) custom-call(s32[1,96]{1,0:T(1,128)} %refs_0_.1, s32[1,96]{1,0:T(1,128)} %refs_1_.1, s32[1,6]{1,0:T(1,128)} %refs_2_.1, s32[1,2,6]{2,1,0:T(2,128)} %refs_3_.1, bf16[960,128]{1,0:T(8,128)(2,1)} %constant.4.clone.refs_4_, bf16[656,256]{1,0:T(8,128)(2,1)} %constant.5.clone.refs_5_, ...), custom_call_target="tpu_custom_call" | custom-call | tf_op jit(solution)/shard_map/pallas_call | solution.py:351
  45.3 0.8 %copy.14 = bf16[1,48,6,6,96]{4,1,3,2,0:T(8,128)(2,1)} copy(bf16[1,48,6,6,96]{4,1,3,2,0:T(8,128)(2,1)S(1)} %bitcast.17) | data formatting | bytes 663552
